TPU v7x, 32 devices: a whole 2x2x4 slice. The times are simulated.
32 devices in a mesh: shots: 2 (over x), mx: 16 (over z, y, core).
Axes of the slice: x: 2, y: 2, z: 4, core: 2. Of those that a mesh axis runs over, the one named last changes fastest.
Arguments:
- initial: float32 [18, 125, 2048], P('shots', None, 'mx'), parts along dimension 0, may hold values from -6 to 6
- derivative: float32 [3, 125, 125], replicated, may hold values from -0.5 to 0.5
- coupling: float32 [3, 9, 9], replicated, may hold values from -2 to 2
- face_lift: float32 [2, 125, 125], replicated, may hold values from -0.5 to 0.5
- metric: float32 [3, 2048], P(None, 'mx'), may hold values from 0.3 to 3
- rec_element: int32 [4096], P('mx'), may hold values from 0 to 127
- rec_weight: float32 [125, 4096], P(None, 'mx'), may hold values from -0.5 to 0.5
- live_counts: int32 [16], replicated, may hold values from 1 to 256, 2048 in all
- shot_order: int32 [4096], replicated, may hold values from 0 to 4095, as said below
- observed: float32 [8192, 48], P(('shots', 'mx')), parts along dimension 0, may hold values from -6 to 6
Outputs:
- residual: float32 [8192, 48], P(('shots', 'mx')), parts along dimension 0
- misfit: float32 [8192], P(('shots', 'mx')), parts along dimension 0
- adjoint: float32 [8192, 48], P(('shots', 'mx')), parts along dimension 0
There are 2 independent parts, one for each index of `shots`. A program takes and returns all parts, laid end to end along the dimension named above; an argument that names none is the same for every part. Nothing has to cross between parts.
Inputs may be any that keep to these rules, and one draw needn't show every extreme that they name: `rec_element`: local element index of the slot within its block of 128 elements. The live receivers of block b are its first live_counts[b] slots. `shot_order`: a permutation of the slots; of the 256 positions of each block of shot-receiver order, exactly 16 come from the slots of each block.
All inputs are finite; a program needn't handle non-finite values.
Results may differ from a plain program's by a relative error of at most 0.00018.
Values sent between devices are 32-bit elements; how exact they have to be, the bound alone decides.
A program may use at most 64 MiB of HBM per device.

v0:
```python
import jax
import jax.numpy as jnp
from jax import lax
from jax.sharding import PartitionSpec as P

STEPS = 12
DEPTH = 4


HIGH = lax.Precision.HIGHEST


def with_halo(block, sides, width):
    for axis, dim in sides:
        count = lax.axis_size(axis)
        forward = [(i, i + 1) for i in range(count - 1)]
        backward = [(target, source) for source, target in forward]
        low = lax.ppermute(
            lax.slice_in_dim(block, block.shape[dim] - width, None, axis=dim), axis, forward
        )
        high = lax.ppermute(lax.slice_in_dim(block, 0, width, axis=dim), axis, backward)
        block = jnp.concatenate([low, block, high], axis=dim)
    return block


def advance(extended, metric_cols, derivative, coupling, face_lift, time_step):
    middle = extended[:, :, 1:-1]
    summed = jnp.einsum("pq,fqe->fpe", face_lift[0], extended[:, :, :-2] - middle, precision=HIGH)
    summed = summed + jnp.einsum(
        "pq,fqe->fpe", face_lift[1], extended[:, :, 2:] - middle, precision=HIGH
    )
    for k in range(3):
        gradient = jnp.einsum("pq,fqe->fpe", derivative[k], middle, precision=HIGH)
        summed = (
            summed
            + jnp.einsum("gf,fpe->gpe", coupling[k], gradient, precision=HIGH)
            * metric_cols[k][None, None, :]
        )
    return middle + time_step * summed


def sample(wavefield, elements, rec_weight, live_slot):
    components = jnp.stack(
        [
            wavefield[0],
            wavefield[1],
            wavefield[2],
            (wavefield[3] + wavefield[4] + wavefield[5]) / 3.0,
        ]
    )
    columns = jnp.take(components, elements, axis=2)
    return jnp.sum(columns * rec_weight[None], axis=1) * live_slot[None]


def shards(
    initial,
    derivative,
    coupling,
    face_lift,
    metric,
    rec_element,
    rec_weight,
    live_counts,
    shot_order,
    observed,
):
    time_step = 0.5 / STEPS
    elem_count = initial.shape[2]
    slot_count = rec_element.shape[0]
    peer_count = lax.axis_size("mx")
    pair_rows = slot_count // peer_count
    my_index = lax.axis_index("mx")
    row_width = 4 * STEPS
    live_slot = (jnp.arange(slot_count, dtype=jnp.int32) < live_counts[my_index]).astype(
        jnp.float32
    )
    by_block = shot_order.reshape(peer_count, slot_count)
    source_blk = by_block // slot_count
    slot_of = by_block % slot_count
    mine = (source_blk == my_index).astype(jnp.int32)
    rank_in = jnp.cumsum(mine, axis=1) - 1
    rank_in = jnp.where(mine > 0, rank_in, pair_rows)
    dest_rows = jnp.broadcast_to(jnp.arange(peer_count, dtype=jnp.int32)[:, None], rank_in.shape)
    send_index = (
        jnp.zeros((peer_count, pair_rows), jnp.int32)
        .at[dest_rows, rank_in]
        .set(slot_of, mode="drop")
    )
    own_source = lax.dynamic_index_in_dim(source_blk, my_index, 0, keepdims=False)
    own_slot = lax.dynamic_index_in_dim(slot_of, my_index, 0, keepdims=False)
    onehot = (own_source[:, None] == jnp.arange(peer_count, dtype=jnp.int32)[None, :]).astype(
        jnp.int32
    )
    running = jnp.cumsum(onehot, axis=0)
    own_rank = jnp.take_along_axis(running, own_source[:, None], axis=1)[:, 0] - 1
    flat_pos = own_source * pair_rows + own_rank
    live_out = (own_slot < live_counts[own_source]).astype(jnp.float32)
    trace_buffer = jnp.zeros((4, STEPS, slot_count), jnp.float32)
    metric_wide = with_halo(metric, (("mx", 1),), DEPTH)
    full_width = elem_count + 2 * DEPTH
    first_cell = my_index * elem_count - DEPTH
    cell_ids = first_cell + jnp.arange(full_width, dtype=jnp.int32)
    inside_mask = ((cell_ids >= 0) & (cell_ids < elem_count * peer_count)).astype(jnp.float32)

    def block_step(b, carry):
        wavefield, record_buf = carry
        extended = with_halo(wavefield, (("mx", 2),), DEPTH)
        for s in range(DEPTH):
            rim_left = DEPTH - 1 - s
            stop_col = full_width - s - 1
            extended = advance(
                extended,
                metric_wide[:, s + 1 : stop_col],
                derivative,
                coupling,
                face_lift,
                time_step,
            )
            extended = extended * inside_mask[None, None, s + 1 : stop_col]
            current = extended[:, :, rim_left : rim_left + elem_count]
            sampled = sample(current, rec_element, rec_weight, live_slot)
            record_buf = lax.dynamic_update_slice(
                record_buf, sampled[:, None, :], (0, b * DEPTH + s, 0)
            )
        return (extended, record_buf)

    final_field, trace_buffer = lax.fori_loop(
        0, STEPS // DEPTH, block_step, (initial, trace_buffer)
    )
    synthetic = trace_buffer.transpose(2, 0, 1).reshape(slot_count, row_width)
    send_buffer = synthetic[send_index]
    received = lax.all_to_all(send_buffer, "mx", split_axis=0, concat_axis=0, tiled=True)
    ordered = received.reshape(peer_count * pair_rows, row_width)[flat_pos]
    residual = live_out[:, None] * (ordered - observed)
    misfit = 0.5 * jnp.sum(residual * residual, axis=1)
    flipped = residual.reshape(slot_count, 4, STEPS)[:, :, ::-1].reshape(slot_count, row_width)
    back_buffer = (
        jnp.zeros((peer_count * pair_rows, row_width), jnp.float32).at[flat_pos].set(flipped)
    )
    returned = lax.all_to_all(
        back_buffer.reshape(peer_count, pair_rows, row_width),
        "mx",
        split_axis=0,
        concat_axis=0,
        tiled=True,
    )
    adjoint = (
        jnp.zeros((slot_count, row_width), jnp.float32)
        .at[send_index.reshape(-1)]
        .set(returned.reshape(peer_count * pair_rows, row_width))
    )
    return (residual, misfit, adjoint)


def solution(mesh):
    in_specs = (
        P("shots", None, "mx"),
        P(),
        P(),
        P(),
        P(None, "mx"),
        P("mx"),
        P(None, "mx"),
        P(),
        P(),
        P(("shots", "mx"), None),
    )
    out_specs = (P(("shots", "mx"), None), P(("shots", "mx")), P(("shots", "mx"), None))
    return jax.shard_map(shards, mesh=mesh, in_specs=in_specs, out_specs=out_specs, check_vma=False)
```

profile of v0, /device:TPU:0, one launch (start us, length us, event | category | flops | bytes accessed | tf_op | source)
XLA Modules:
  0.0 321.7 jit_solution(3316549150153748987)
XLA Ops:
  1.5 2.4 collective-permute-start.2
  9.2 2.0 fusion.179
  11.3 4.5 %compare_select_fusion.7 = (s32[256,1]{0,1:T(1,128)S(1)}, s32[256,1]{0,1:T(1,128)S(1)}, s32[1,256]{1,0:T(1,128)S(1)}) fusion(s32[]{:T(128)} %bitcast.11, s32[]{:T(128)} %bitcast.12, s32[]{:T(128)} %bitcast.13, s32[]{:T(128)} %bitcast.14, s32[]{:T(128)} %bitcast.15, s32[]{:T(128)} %bitcast.17, s32[]{:T(128)} %bitcast.16, ...), kind=kLoop, calls=%fused_computation.282 | loop fusion | flops 5888 | bytes 5664 | tf_op jit(solution)/shard_map/gather | solution.py:97
  15.9 15.5 %scatter_custom_fusion.2 = s32[256]{0:T(256)S(1)} fusion(s32[4096]{0:T(1024)S(1)} %bitcast.471, s32[4096]{0:T(1024)S(1)} %bitcast.472, s32[]{:T(128)} %constant.196.clone.1), kind=kCustom, calls=%fused_computation.304 | custom fusion | bytes 1028
  33.7 2.4 gather_fusion.6
  38.5 6.3 %compare_convert_fusion.1 = f32[256]{0:T(256)} fusion(s32[256]{0:T(256)S(1)} %bitcast.474, pred[256]{0:T(512)(128)(4,1)S(1)} %get-tuple-element.377, pred[256]{0:T(512)(128)(4,1)S(1)} %get-tuple-element.375, pred[256]{0:T(512)(128)(4,1)S(1)} %get-tuple-element.376, pred[256]{0:T(512)(128)(4,1)S(1)} %get-tuple-element.374, ...), kind=kLoop, calls=%fused_computation.291 | loop fusion | flops 2816 | bytes 5412 | tf_op jit(solution)/shard_map/convert_element_type | solution.py:97
  46.8 237.1 %while.18 = (s32[]{:T(128)}, f32[9,125,128]{1,2,0:T(8,128)S(1)}, f32[4,12,256]{0,2,1:T(8,128)}, f32[2,125,125]{2,1,0:T(8,128)S(1)}, f32[3,125,125]{2,1,0:T(8,128...) while((s32[]{:T(128)}, f32[9,125,128]{1,2,0:T(8,128)S(1)}, ...), condition=%wide.region_5.7_spmd.clone, body=%wide.region_0.6_spmd.clone.sunk | while | flops 4621616640 | bytes 95879024 | solution.py:127
  48.3 5.8 %collective-permute-start.1 = (f32[9,125,4]{1,2,0:T(4,128)S(1)}, f32[9,125,4]{1,2,0:T(4,128)S(1)}, u32[]{:S(2)}, u32[]{:S(2)}) collective-permute-start(f32[9,125,4]{1,2,0:T(4,128)S(1)} %get-tuple-element.538), channel_id=1, source_target_pairs={{0,1},{1,2},{2,3},{3,4},{4,5},{5,6},{6,7},{7,8},{8,9},{9,10},{10,1... | collective-permute-start | bytes 54008 | tf_op jit(solution)/shard_map/while/body/eval_jaxpr/ppermute | solution.py:18
  58.0 1.9 compare_and_fusion.2
  69.6 2.0 fusion.334
  81.0 2.0 fusion.340
  92.5 2.1 fusion.346
  109.4 3.0 fusion.351
  119.6 3.1 fusion.356
  127.5 4.3 %collective-permute-start.1 = (f32[9,125,4]{1,2,0:T(4,128)S(1)}, f32[9,125,4]{1,2,0:T(4,128)S(1)}, u32[]{:S(2)}, u32[]{:S(2)}) collective-permute-start(f32[9,125,4]{1,2,0:T(4,128)S(1)} %get-tuple-element.538), channel_id=1, source_target_pairs={{0,1},{1,2},{2,3},{3,4},{4,5},{5,6},{6,7},{7,8},{8,9},{9,10},{10,1... | collective-permute-start | bytes 54008 | tf_op jit(solution)/shard_map/while/body/eval_jaxpr/ppermute | solution.py:18
  135.6 1.9 compare_and_fusion.2
  147.2 2.0 fusion.334
  158.3 2.0 fusion.340
  169.9 2.1 fusion.346
  187.0 3.0 fusion.351
  197.1 3.1 fusion.356
  204.8 4.3 %collective-permute-start.1 = (f32[9,125,4]{1,2,0:T(4,128)S(1)}, f32[9,125,4]{1,2,0:T(4,128)S(1)}, u32[]{:S(2)}, u32[]{:S(2)}) collective-permute-start(f32[9,125,4]{1,2,0:T(4,128)S(1)} %get-tuple-element.538), channel_id=1, source_target_pairs={{0,1},{1,2},{2,3},{3,4},{4,5},{5,6},{6,7},{7,8},{8,9},{9,10},{10,1... | collective-permute-start | bytes 54008 | tf_op jit(solution)/shard_map/while/body/eval_jaxpr/ppermute | solution.py:18
  224.6 2.0 fusion.334
  235.9 2.0 fusion.340
  247.4 2.1 fusion.346
  264.3 3.0 fusion.351
  274.5 3.1 fusion.356
  283.9 2.0 copy.97
  287.6 9.0 %all-to-all-start = ((f32[16,1,768]{2,1,0:T(1,128)}), f32[16,1,768]{2,1,0:T(1,128)S(1)}, u32[]{:S(2)}, u32[]{:S(2)}) async-start(f32[16,1,768]{2,1,0:T(1,128)} %reshape.732), calls=%async_computation | async-start | bytes 98304 | tf_op jit(solution)/shard_map/all_to_all | solution.py:132
  296.6 6.7 %all-to-all-done = f32[16,1,768]{2,1,0:T(1,128)S(1)} async-done(((f32[16,1,768]{2,1,0:T(1,128)}), f32[16,1,768]{2,1,0:T(1,128)S(1)}, u32[]{:S(2)}, u32[]{:S(2)}) %all-to-all-start) | async-done | bytes 49184 | tf_op jit(solution)/shard_map/all_to_all | solution.py:132
  308.0 3.5 %all-to-all-start.1 = ((f32[16,1,768]{2,1,0:T(1,128)}), f32[16,1,768]{2,1,0:T(1,128)S(1)}, u32[]{:S(2)}, u32[]{:S(2)}) async-start(f32[16,1,768]{2,1,0:T(1,128)} %reshape.734), calls=%async_computation.1 | async-start | bytes 98304 | tf_op jit(solution)/shard_map/all_to_all | solution.py:140
  312.1 6.2 %all-to-all-done.1 = f32[16,1,768]{2,1,0:T(1,128)S(1)} async-done(((f32[16,1,768]{2,1,0:T(1,128)}), f32[16,1,768]{2,1,0:T(1,128)S(1)}, u32[]{:S(2)}, u32[]{:S(2)}) %all-to-all-start.1) | async-done | bytes 49184 | tf_op jit(solution)/shard_map/all_to_all | solution.py:140
  (436 shorter events, 199.0 us)
Async XLA Ops:
  0.6 36.0 %copy-start.28 = (f32[3,9,9]{2,0,1:T(4,128)S(1)}, f32[3,9,9]{2,0,1:T(4,128)}, u32[]{:S(2)}) copy-start(f32[3,9,9]{2,0,1:T(4,128)} %param.16) | copy-start | bytes 2920
  0.6 36.0 %copy-start.19 = (f32[2,125,125]{2,0,1:T(2,128)S(1)}, f32[2,125,125]{2,0,1:T(2,128)}, u32[]{:S(2)}) copy-start(f32[2,125,125]{2,0,1:T(2,128)} %param.17) | copy-start | bytes 375004
  1.5 43.3 %collective-permute-start.2 = (f32[3,4]{1,0:T(4,128)S(1)}, f32[3,4]{1,0:T(4,128)S(1)}, u32[]{:S(2)}, u32[]{:S(2)}) collective-permute-start(f32[3,4]{1,0:T(4,128)S(1)} %get-tuple-element.425), channel_id=1, source_target_pairs={{0,1},{1,2},{2,3},{3,4},{4,5},{5,6},{6,7},{7,8},{8,9},{9,10},{10,1... | collective-permute-start | bytes 152 | tf_op jit(solution)/shard_map/ppermute | solution.py:18
  3.9 40.9 %collective-permute-start.3 = (f32[3,4]{1,0:T(4,128)S(1)}, f32[3,4]{1,0:T(4,128)S(1)}, u32[]{:S(2)}, u32[]{:S(2)}) collective-permute-start(f32[3,4]{1,0:T(4,128)S(1)} %get-tuple-element.426), channel_id=1, source_target_pairs={{1,0},{2,1},{3,2},{4,3},{5,4},{6,5},{7,6},{8,7},{9,8},{10,9},{11,1... | collective-permute-start | bytes 152 | tf_op jit(solution)/shard_map/ppermute | solution.py:21
  6.7 30.0 %copy-start.18 = (f32[125,256]{1,0:T(8,128)S(1)}, f32[125,256]{1,0:T(8,128)}, u32[]{:S(2)}) copy-start(f32[125,256]{1,0:T(8,128)} %param.20) | copy-start | bytes 384004
  8.4 29.0 %copy-start.26 = (f32[256,48]{0,1:T(8,128)S(1)}, f32[256,48]{0,1:T(8,128)}, u32[]{:S(2)}) copy-start(f32[256,48]{0,1:T(8,128)} %param.23) | copy-start | bytes 147460
  11.3 27.0 %copy-start.12 = (f32[9,125,128]{2,1,0:T(8,128)S(1)}, f32[9,125,128]{2,1,0:T(8,128)}, u32[]{:S(2)}) copy-start(f32[9,125,128]{2,1,0:T(8,128)} %param.14) | copy-start | bytes 1728004
  36.1 8.7 %copy-start.20 = (f32[3,128]{1,0:T(4,128)S(1)}, f32[3,128]{1,0:T(4,128)}, u32[]{:S(2)}) copy-start(f32[3,128]{1,0:T(4,128)} %param.18) | copy-start | bytes 4612
  38.5 8.3 %copy-start = (f32[3,125,125]{2,1,0:T(8,128)S(1)}, f32[3,125,125]{2,1,0:T(8,128)}, u32[]{:S(2)}) copy-start(f32[3,125,125]{2,1,0:T(8,128)} %param.15) | copy-start | bytes 562504
  47.0 15.6 %copy-start.15 = (f32[136]{0:T(256)}, f32[136]{0:T(256)S(1)}, u32[]{:S(2)}) copy-start(f32[136]{0:T(256)S(1)} %get-tuple-element.606) | copy-start | bytes 1636 | tf_op jit(solution)/shard_map/while
  47.0 51.7 %copy-start.3 = (f32[2,125,125]{2,1,0:T(8,128)}, f32[2,125,125]{2,1,0:T(8,128)S(1)}, u32[]{:S(2)}) copy-start(f32[2,125,125]{2,1,0:T(8,128)S(1)} %get-tuple-element.602) | copy-start | bytes 375004 | tf_op jit(solution)/shard_map/while
  47.0 14.3 %collective-permute-start = (f32[9,125,4]{1,2,0:T(4,128)S(1)}, f32[9,125,4]{1,2,0:T(4,128)S(1)}, u32[]{:S(2)}, u32[]{:S(2)}) collective-permute-start(f32[9,125,4]{1,2,0:T(4,128)S(1)} %get-tuple-element.537), channel_id=1, source_target_pairs={{1,0},{2,1},{3,2},{4,3},{5,4},{6,5},{7,6},{8,7},{9,8},{10,9},{11,1... | collective-permute-start | bytes 54008 | tf_op jit(solution)/shard_map/while/body/eval_jaxpr/ppermute | solution.py:21
  48.3 13.0 %collective-permute-start.1 = (f32[9,125,4]{1,2,0:T(4,128)S(1)}, f32[9,125,4]{1,2,0:T(4,128)S(1)}, u32[]{:S(2)}, u32[]{:S(2)}) collective-permute-start(f32[9,125,4]{1,2,0:T(4,128)S(1)} %get-tuple-element.538), channel_id=1, source_target_pairs={{0,1},{1,2},{2,3},{3,4},{4,5},{5,6},{6,7},{7,8},{8,9},{9,10},{10,1... | collective-permute-start | bytes 54008 | tf_op jit(solution)/shard_map/while/body/eval_jaxpr/ppermute | solution.py:18
  119.6 6.1 %copy-start.4 = (f32[2,125,125]{2,1,0:T(8,128)S(1)}, f32[2,125,125]{2,1,0:T(8,128)}, u32[]{:S(2)}) copy-start(f32[2,125,125]{2,1,0:T(8,128)} %copy-done.3) | copy-start | bytes 375004 | tf_op jit(solution)/shard_map/while
  119.6 6.1 %copy-start.5 = (f32[9,125,128]{1,2,0:T(8,128)S(1)}, f32[9,125,128]{1,2,0:T(8,128)}, u32[]{:S(2)}) copy-start(f32[9,125,128]{1,2,0:T(8,128)} %fusion.351) | copy-start | bytes 1728004 | tf_op jit(solution)/shard_map/while
  126.1 14.1 %copy-start.15 = (f32[136]{0:T(256)}, f32[136]{0:T(256)S(1)}, u32[]{:S(2)}) copy-start(f32[136]{0:T(256)S(1)} %get-tuple-element.606) | copy-start | bytes 1636 | tf_op jit(solution)/shard_map/while
  126.1 49.9 %copy-start.3 = (f32[2,125,125]{2,1,0:T(8,128)}, f32[2,125,125]{2,1,0:T(8,128)S(1)}, u32[]{:S(2)}) copy-start(f32[2,125,125]{2,1,0:T(8,128)S(1)} %get-tuple-element.602) | copy-start | bytes 375004 | tf_op jit(solution)/shard_map/while
  126.2 12.8 %collective-permute-start = (f32[9,125,4]{1,2,0:T(4,128)S(1)}, f32[9,125,4]{1,2,0:T(4,128)S(1)}, u32[]{:S(2)}, u32[]{:S(2)}) collective-permute-start(f32[9,125,4]{1,2,0:T(4,128)S(1)} %get-tuple-element.537), channel_id=1, source_target_pairs={{1,0},{2,1},{3,2},{4,3},{5,4},{6,5},{7,6},{8,7},{9,8},{10,9},{11,1... | collective-permute-start | bytes 54008 | tf_op jit(solution)/shard_map/while/body/eval_jaxpr/ppermute | solution.py:21
  127.5 11.5 %collective-permute-start.1 = (f32[9,125,4]{1,2,0:T(4,128)S(1)}, f32[9,125,4]{1,2,0:T(4,128)S(1)}, u32[]{:S(2)}, u32[]{:S(2)}) collective-permute-start(f32[9,125,4]{1,2,0:T(4,128)S(1)} %get-tuple-element.538), channel_id=1, source_target_pairs={{0,1},{1,2},{2,3},{3,4},{4,5},{5,6},{6,7},{7,8},{8,9},{9,10},{10,1... | collective-permute-start | bytes 54008 | tf_op jit(solution)/shard_map/while/body/eval_jaxpr/ppermute | solution.py:18
  197.1 6.1 %copy-start.4 = (f32[2,125,125]{2,1,0:T(8,128)S(1)}, f32[2,125,125]{2,1,0:T(8,128)}, u32[]{:S(2)}) copy-start(f32[2,125,125]{2,1,0:T(8,128)} %copy-done.3) | copy-start | bytes 375004 | tf_op jit(solution)/shard_map/while
  197.1 6.1 %copy-start.5 = (f32[9,125,128]{1,2,0:T(8,128)S(1)}, f32[9,125,128]{1,2,0:T(8,128)}, u32[]{:S(2)}) copy-start(f32[9,125,128]{1,2,0:T(8,128)} %fusion.351) | copy-start | bytes 1728004 | tf_op jit(solution)/shard_map/while
  203.4 14.1 %copy-start.15 = (f32[136]{0:T(256)}, f32[136]{0:T(256)S(1)}, u32[]{:S(2)}) copy-start(f32[136]{0:T(256)S(1)} %get-tuple-element.606) | copy-start | bytes 1636 | tf_op jit(solution)/shard_map/while
  203.5 50.1 %copy-start.3 = (f32[2,125,125]{2,1,0:T(8,128)}, f32[2,125,125]{2,1,0:T(8,128)S(1)}, u32[]{:S(2)}) copy-start(f32[2,125,125]{2,1,0:T(8,128)S(1)} %get-tuple-element.602) | copy-start | bytes 375004 | tf_op jit(solution)/shard_map/while
  203.5 12.8 %collective-permute-start = (f32[9,125,4]{1,2,0:T(4,128)S(1)}, f32[9,125,4]{1,2,0:T(4,128)S(1)}, u32[]{:S(2)}, u32[]{:S(2)}) collective-permute-start(f32[9,125,4]{1,2,0:T(4,128)S(1)} %get-tuple-element.537), channel_id=1, source_target_pairs={{1,0},{2,1},{3,2},{4,3},{5,4},{6,5},{7,6},{8,7},{9,8},{10,9},{11,1... | collective-permute-start | bytes 54008 | tf_op jit(solution)/shard_map/while/body/eval_jaxpr/ppermute | solution.py:21
  204.8 11.5 %collective-permute-start.1 = (f32[9,125,4]{1,2,0:T(4,128)S(1)}, f32[9,125,4]{1,2,0:T(4,128)S(1)}, u32[]{:S(2)}, u32[]{:S(2)}) collective-permute-start(f32[9,125,4]{1,2,0:T(4,128)S(1)} %get-tuple-element.538), channel_id=1, source_target_pairs={{0,1},{1,2},{2,3},{3,4},{4,5},{5,6},{6,7},{7,8},{8,9},{9,10},{10,1... | collective-permute-start | bytes 54008 | tf_op jit(solution)/shard_map/while/body/eval_jaxpr/ppermute | solution.py:18
  274.5 6.1 %copy-start.4 = (f32[2,125,125]{2,1,0:T(8,128)S(1)}, f32[2,125,125]{2,1,0:T(8,128)}, u32[]{:S(2)}) copy-start(f32[2,125,125]{2,1,0:T(8,128)} %copy-done.3) | copy-start | bytes 375004 | tf_op jit(solution)/shard_map/while
  286.0 10.7 %copy-start.31 = (s32[256,1]{0,1:T(1,128)S(1)}, s32[256,1]{0,1:T(1,128)}, u32[]{:S(2)}) copy-start(s32[256,1]{0,1:T(1,128)} %compare_select_fusion.4) | copy-start | bytes 3076
  286.8 18.7 %copy-start.13 = (f32[256,48]{1,0:T(8,128)S(1)}, f32[256,48]{1,0:T(8,128)}, u32[]{:S(2)}) copy-start(f32[256,48]{1,0:T(8,128)} %copy.105) | copy-start | bytes 147460
  286.8 18.7 %copy-start.30 = (f32[256]{0:T(256)S(1)}, f32[256]{0:T(256)}, u32[]{:S(2)}) copy-start(f32[256]{0:T(256)} %compare_convert_fusion.1) | copy-start | bytes 3076
  287.6 15.8 %all-to-all-start = ((f32[16,1,768]{2,1,0:T(1,128)}), f32[16,1,768]{2,1,0:T(1,128)S(1)}, u32[]{:S(2)}, u32[]{:S(2)}) async-start(f32[16,1,768]{2,1,0:T(1,128)} %reshape.732), calls=%async_computation | async-start | bytes 98304 | tf_op jit(solution)/shard_map/all_to_all | solution.py:132
  305.8 15.3 %copy-start.17 = (f32[256,48]{0,1:T(8,128)}, f32[256,48]{0,1:T(8,128)S(1)}, u32[]{:S(2)}) copy-start(f32[256,48]{0,1:T(8,128)S(1)} %copy.108) | copy-start | bytes 147460
  308.0 10.2 %all-to-all-start.1 = ((f32[16,1,768]{2,1,0:T(1,128)}), f32[16,1,768]{2,1,0:T(1,128)S(1)}, u32[]{:S(2)}, u32[]{:S(2)}) async-start(f32[16,1,768]{2,1,0:T(1,128)} %reshape.734), calls=%async_computation.1 | async-start | bytes 98304 | tf_op jit(solution)/shard_map/all_to_all | solution.py:140
  (50 other events, 116.2 us)
where the time goes:
time: 326 us; the launch traced here: 322 us
  matrix products  124 us (38%)
  local copies, waits for them, and re-layouts  89.5 us (27%)
  other arithmetic  53.6 us (16%)
  starting transfers between devices  34.4 us (11%)
  waiting for transfers between devices  12.9 us (4%)
  loops' own time  5.81 us (2%)
    dot_general x36, matrix products, advance(): jnp.einsum('gf,fpe->gpe', coupling[k], gradient, precision=HIGH)  41 us
    dot_general x36, matrix products, advance(): gradient = jnp.einsum('pq,fqe->fpe', derivative[k], middle, precision=HIGH)  40.8 us
    dot_general x12, matrix products, advance(): jnp.einsum('pq,fqe->fpe', face_lift[1], extended[:, :, 2:] - middle, prec...  24.6 us
    unnamed x39, local copies, waits for them, and re-layouts  19.9 us
    dot_general x12, matrix products, advance(): jnp.einsum('pq,fqe->fpe', face_lift[0], extended[:, :, :-2] - middle, pre...  17.4 us
    ppermute x4, starting transfers between devices, with_halo(): lax.ppermute(lax.slice_in_dim(block, block.shape[dim] - width, None, axis...  16.7 us
    gather x12, local copies, waits for them, and re-layouts, sample(): columns = jnp.take(components, elements, axis=2)  11.9 us
    dot_general x9, local copies, waits for them, and re-layouts, advance(): jnp.einsum('gf,fpe->gpe', coupling[k], gradient, precision=HIGH)  10.4 us
  transfers between devices with their start and end apart: 10, of which 2 were waited for; matrix products, arithmetic and copies ran while one was open for 19% of the time, Pallas kernels for 0%

commit v1 on v0

v1 whole, which is shorter than its diff:
```python
import functools
import jax
import jax.numpy as jnp
from jax import lax
from jax.experimental import pallas as pl
from jax.experimental.pallas import tpu as pltpu
from jax.sharding import PartitionSpec as P

STEPS = 12
COMPS = 4
HALO = 16
GUARD = 8
HIGH = lax.Precision.HIGHEST


def split(x):
    hi = x.astype(jnp.bfloat16)
    return hi, (x - hi.astype(jnp.float32)).astype(jnp.bfloat16)


def wave_kernel(own, low, high, metric, mask, wmat, weight, elem, live, cpl, out, ubuf, lhs, wb, ws, hist):
    fields, count, lanes = own.shape
    first = GUARD + HALO
    kdim = wmat.shape[0]
    rows_all = ubuf.shape[2]
    for b in range(2):
        for f in range(fields):
            ubuf[b, f] = jnp.zeros((rows_all, lanes), jnp.float32)
    for f in range(fields):
        ubuf[0, f, GUARD:first] = low[f]
        ubuf[0, f, first:first + count] = own[f]
        ubuf[0, f, first + count:first + count + HALO] = high[f]
    for k in range(kdim // lanes):
        hi, lo = split(wmat[k * lanes:(k + 1) * lanes])
        for base in (0, kdim):
            wb[base + k * lanes:base + (k + 1) * lanes, :lanes] = hi
            wb[base + k * lanes:base + (k + 1) * lanes, lanes:] = lo
    hi, lo = split(weight[...])
    ws[0:lanes] = hi
    ws[lanes:2 * lanes] = hi
    ws[2 * lanes:] = lo

    def mix(src, c, halo, slab):
        rows = count + 2 * halo
        base = first - halo
        for gi in range(3):
            g = c * 3 + gi
            for r in range(0, rows, slab):
                acc = [None] * 3
                for f in range(fields):
                    uf = ubuf[src, f, base + r:base + r + slab]
                    for k in range(3):
                        term = cpl[(k * fields + g) * fields + f] * uf
                        acc[k] = term if acc[k] is None else acc[k] + term
                at = gi * rows + r
                mid = ubuf[src, g, base + r:base + r + slab]
                vals = [acc[k] * metric[k, HALO - halo + r:HALO - halo + r + slab] for k in range(3)]
                vals.append(ubuf[src, g, base + r - 1:base + r - 1 + slab] - mid)
                vals.append(ubuf[src, g, base + r + 1:base + r + 1 + slab] - mid)
                for k, v in enumerate(vals):
                    hi, lo = split(v)
                    lhs[c, at:at + slab, k * lanes:(k + 1) * lanes] = hi
                    lhs[c, at:at + slab, kdim + k * lanes:kdim + (k + 1) * lanes] = lo

    def apply(src, dst, c, halo):
        rows = count + 2 * halo
        base = first - halo
        res = jnp.dot(lhs[c, :3 * rows], wb[...], preferred_element_type=jnp.float32)
        for gi in range(3):
            g = c * 3 + gi
            part = res[gi * rows:(gi + 1) * rows]
            new = ubuf[src, g, base:base + rows] + (part[:, :lanes] + part[:, lanes:])
            ubuf[dst, g, base:base + rows] = new * mask[HALO - halo:HALO - halo + rows]

    def step(halo, slab, t, _):
        src = lax.rem(t, 2)
        dst = 1 - src
        mix(src, 0, halo, slab)
        mix(src, 1, halo, slab)
        apply(src, dst, 0, halo)
        mix(src, 2, halo, slab)
        apply(src, dst, 1, halo)
        apply(src, dst, 2, halo)
        mine = slice(first, first + count)
        vals = [ubuf[dst, c, mine] for c in range(3)]
        vals.append((ubuf[dst, 3, mine] + ubuf[dst, 4, mine] + ubuf[dst, 5, mine]) / 3.0)
        for c, v in enumerate(vals):
            hi, lo = split(v)
            hist[t, c, :, 0:lanes] = hi
            hist[t, c, :, lanes:2 * lanes] = lo
            hist[t, c, :, 2 * lanes:] = hi
        return 0

    lax.fori_loop(0, 3, functools.partial(step, 16, 80), 0)
    lax.fori_loop(3, STEPS, functools.partial(step, 8, 48), 0)

    slots = weight.shape[1]
    ids = lax.broadcasted_iota(jnp.int32, (count, slots), 0)
    pick = jnp.where(ids == elem[...], live[...], 0.0)

    def sample(t, _):
        for c in range(COMPS):
            prod = jnp.dot(hist[t, c], ws[...], preferred_element_type=jnp.float32)
            out[pl.ds(c * STEPS + t, 1), :] = jnp.sum(prod * pick, axis=0, keepdims=True)
        return 0

    lax.fori_loop(0, STEPS, sample, 0)


def waves(own, low, high, metric, mask, wmat, weight, elem, live, cpl):
    fields, count, lanes = own.shape
    slots = weight.shape[1]
    vm = pl.BlockSpec(memory_space=pltpu.VMEM)
    return pl.pallas_call(
        wave_kernel,
        out_shape=jax.ShapeDtypeStruct((COMPS * STEPS, slots), jnp.float32),
        in_specs=[vm] * 9 + [pl.BlockSpec(memory_space=pltpu.SMEM)],
        out_specs=vm,
        scratch_shapes=[
            pltpu.VMEM((2, fields, count + 2 * (HALO + GUARD), lanes), jnp.float32),
            pltpu.VMEM((3, 3 * (count + 2 * HALO), 2 * wmat.shape[0]), jnp.bfloat16),
            pltpu.VMEM((2 * wmat.shape[0], 2 * lanes), jnp.bfloat16),
            pltpu.VMEM((3 * lanes, slots), jnp.bfloat16),
            pltpu.VMEM((STEPS, COMPS, count, 3 * lanes), jnp.bfloat16),
        ],
        cost_estimate=pl.CostEstimate(flops=10**10, bytes_accessed=2 * 10**6, transcendentals=0),
        name="waves",
    )(own, low, high, metric, mask, wmat, weight, elem, live, cpl)


def flip(rows):
    return rows.reshape(-1, COMPS, STEPS)[:, :, ::-1].reshape(-1, COMPS * STEPS)


def shards(initial, derivative, coupling, face_lift, metric, rec_element, rec_weight, live_counts, shot_order, observed):
    time_step = 0.5 / STEPS
    fields, nodes, elems = initial.shape
    lanes = -(-nodes // 128) * 128
    slots = rec_element.shape[0]
    peers = lax.axis_size("mx")
    pair = slots // peers
    me = lax.axis_index("mx")
    up = [(i, i + 1) for i in range(peers - 1)]
    down = [(b, a) for a, b in up]
    pad = lanes - nodes

    own = jnp.pad(initial.transpose(0, 2, 1), ((0, 0), (0, 0), (0, pad)))
    met = metric.T
    low = lax.ppermute(own[:, elems - HALO:], "mx", up)
    high = lax.ppermute(own[:, :HALO], "mx", down)
    met_low = lax.ppermute(met[elems - HALO:], "mx", up)
    met_high = lax.ppermute(met[:HALO], "mx", down)
    met_all = jnp.concatenate([met_low, met, met_high], axis=0).T
    met_wide = jnp.broadcast_to(met_all[:, :, None], met_all.shape + (lanes,))
    ids = me * elems - HALO + jnp.arange(elems + 2 * HALO, dtype=jnp.int32)
    inside = ((ids >= 0) & (ids < elems * peers)).astype(jnp.float32)
    inside = jnp.broadcast_to(inside[:, None], (elems + 2 * HALO, lanes))
    mats = jnp.concatenate([derivative, face_lift], axis=0).transpose(0, 2, 1) * time_step
    wmat = jnp.pad(mats, ((0, 0), (0, pad), (0, pad))).reshape(-1, lanes)
    weight = jnp.pad(rec_weight, ((0, pad), (0, 0)))

    slot_ids = jnp.arange(slots, dtype=jnp.int32)
    live = (slot_ids < live_counts[me]).astype(jnp.float32)
    by_block = shot_order.reshape(peers, slots)
    source, slot = by_block // slots, by_block % slots
    tri = (slot_ids[:, None] <= slot_ids[None, :]).astype(jnp.float32)
    mine = source == me
    rank = jnp.dot(mine.astype(jnp.float32), tri).astype(jnp.int32) - 1
    hit = mine[:, None, :] & (rank[:, None, :] == jnp.arange(pair, dtype=jnp.int32)[None, :, None])
    send_slot = jnp.sum(jnp.where(hit, slot[:, None, :], 0), axis=2).reshape(-1)
    to_send = (send_slot[:, None] == slot_ids[None, :]).astype(jnp.float32)
    own_source = lax.dynamic_index_in_dim(source, me, 0, keepdims=False)
    own_slot = lax.dynamic_index_in_dim(slot, me, 0, keepdims=False)
    from_peer = own_source[None, :] == jnp.arange(peers, dtype=jnp.int32)[:, None]
    count = jnp.dot(from_peer.astype(jnp.float32), tri).astype(jnp.int32) - 1
    own_rank = jnp.sum(jnp.where(from_peer, count, 0), axis=0)
    place = own_source * pair + own_rank
    to_place = (place[:, None] == slot_ids[None, :]).astype(jnp.float32)
    own_counts = jnp.sum(jnp.where(from_peer, live_counts[:, None], 0), axis=0)
    live_out = (own_slot < own_counts).astype(jnp.float32)

    def exchange(rows):
        moved = lax.all_to_all(rows.reshape(peers, pair, -1), "mx", split_axis=0, concat_axis=0, tiled=True)
        return moved.reshape(slots, -1)

    sorted_obs = jnp.dot(to_place.T, observed, precision=HIGH)
    slot_obs = jnp.dot(to_send.T, exchange(sorted_obs), precision=HIGH)

    traces = waves(own, low, high, met_wide, inside, wmat, weight, rec_element[None, :], live[None, :], coupling.reshape(-1))
    synthetic = traces.T
    packed = lax.dot_general(to_send, traces, (((1,), (1,)), ((), ())), precision=HIGH)
    ordered = jnp.dot(to_place, exchange(packed), precision=HIGH)
    residual = live_out[:, None] * (ordered - observed)
    misfit = 0.5 * jnp.sum(residual * residual, axis=1)
    adjoint = live[:, None] * flip(synthetic - slot_obs)
    return residual, misfit, adjoint


def solution(mesh):
    in_specs = (
        P("shots", None, "mx"),
        P(),
        P(),
        P(),
        P(None, "mx"),
        P("mx"),
        P(None, "mx"),
        P(),
        P(),
        P(("shots", "mx"), None),
    )
    out_specs = (P(("shots", "mx"), None), P(("shots", "mx")), P(("shots", "mx"), None))
    return jax.shard_map(shards, mesh=mesh, in_specs=in_specs, out_specs=out_specs, check_vma=False)
```

time: 326 us -> 87.8 us (0.27); the launches traced: 322 us -> 87.1 us
  matrix products: 124 us -> 3.07 us
  local copies, waits for them, and re-layouts: 89.5 us -> 11.9 us
  other arithmetic: 53.6 us -> 5.18 us
  Pallas kernels: 0 us -> 38.2 us
  starting transfers between devices: 34.4 us -> 24.1 us
  waiting for transfers between devices: 12.9 us -> 3.61 us
  loops' own time: 5.81 us -> 0 us
    dot_general x96 -> x6, matrix products: 124 us -> 3.07 us  [the longest x1 1.1 us: shards(): lax.dot_general(to_send, traces, (((1,), (1,)), ((), ())), precision=HIGH)]
    pallas_call x0 -> x1, Pallas kernels: none -> 38.2 us  [waves(): pl.pallas_call(wave_kernel, out_shape=jax.ShapeDtypeStruct((COMPS * STEPS...]
    slice x37 -> x2, local copies, waits for them, and re-layouts: 20.2 us -> 0.09 us  [the longest x1 0.07 us: shards(): met_low = lax.ppermute(met[elems - HALO:], 'mx', up)]
    gather x16 -> x0, local copies, waits for them, and re-layouts: 17.8 us -> none  [the longest x12 11.9 us: sample(): columns = jnp.take(components, elements, axis=2)]
    unnamed x39 -> x30, local copies, waits for them, and re-layouts: 19.9 us -> 6.03 us
    ppermute x8 -> x4, starting transfers between devices: 21.9 us -> 10.8 us  [the longest x1 5.78 us: shards(): met_low = lax.ppermute(met[elems - HALO:], 'mx', up)]
    dot_general x9 -> x0, local copies, waits for them, and re-layouts: 10.4 us -> none  [advance(): jnp.einsum('gf,fpe->gpe', coupling[k], gradient, precision=HIGH)]
    transpose x10 -> x0, local copies, waits for them, and re-layouts: 9.64 us -> none  [the longest x9 7.6 us: advance(): gradient = jnp.einsum('pq,fqe->fpe', derivative[k], middle, precision=HIGH)]
  transfers between devices with their start and end apart: 10 -> 6, of which waited for: 2 -> 1; matrix products, arithmetic and copies ran while one was open for 19% -> 16% of each run, Pallas kernels for 0% -> 44%
where the time goes in v1:
time: 87.8 us; the launch traced here: 87.1 us
  Pallas kernels  38.2 us (44%)
  starting transfers between devices  24.1 us (27%)
  local copies, waits for them, and re-layouts  11.9 us (14%)
  other arithmetic  5.18 us (6%)
  waiting for transfers between devices  3.61 us (4%)
  matrix products  3.07 us (3%)
  between operations  0.94 us (1%)
    pallas_call x1, Pallas kernels, waves(): pl.pallas_call(wave_kernel, out_shape=jax.ShapeDtypeStruct((COMPS * STEPS...  38.2 us
    all_to_all x2, starting transfers between devices, exchange(): lax.all_to_all(rows.reshape(peers, pair, -1), 'mx', split_axis=0, concat_...  13.3 us
    unnamed x30, local copies, waits for them, and re-layouts  6.03 us
    ppermute x1, starting transfers between devices, shards(): met_low = lax.ppermute(met[elems - HALO:], 'mx', up)  5.78 us
    all_to_all x2, waiting for transfers between devices, exchange(): lax.all_to_all(rows.reshape(peers, pair, -1), 'mx', split_axis=0, concat_...  3.6 us
    ppermute x1, starting transfers between devices, shards(): low = lax.ppermute(own[:, elems - HALO:], 'mx', up)  2.4 us
    convert_element_type x2, other arithmetic, shards(): live = (slot_ids < live_counts[me]).astype(jnp.float32)  1.86 us
  transfers between devices with their start and end apart: 6, of which 1 were waited for; matrix products, arithmetic and copies ran while one was open for 16% of the time, Pallas kernels for 44%

profile of v1, /device:TPU:0, one launch (start us, length us, event | category | flops | bytes accessed | tf_op | source)
XLA Modules:
  0.0 87.1 jit_solution(2836846627612054040)
XLA Ops:
  0.6 1.3 %copy.22 = f32[9,125,128]{1,2,0:T(8,128)S(1)} copy(f32[9,125,128]{2,1,0:T(8,128)} %param.10) | data formatting | bytes 1152000 | tf_op args[0]
  2.0 2.4 %collective-permute-start = (f32[9,16,128]{2,1,0:T(8,128)S(1)}, f32[9,16,128]{2,1,0:T(8,128)S(1)}, u32[]{:S(2)}, u32[]{:S(2)}) collective-permute-start(f32[9,16,128]{2,1,0:T(8,128)S(1)} %get-tuple-element.6), channel_id=1, source_target_pairs={{0,1},{1,2},{2,3},{3,4},{4,5},{5,6},{6,7},{7,8},{8,9},{9,10},{10,1... | collective-permute-start | bytes 221192 | tf_op jit(solution)/shard_map/ppermute | solution.py:149
  4.4 1.3 %collective-permute-start.1 = (f32[9,16,128]{2,1,0:T(8,128)S(1)}, f32[9,16,128]{2,1,0:T(8,128)S(1)}, u32[]{:S(2)}, u32[]{:S(2)}) collective-permute-start(f32[9,16,128]{2,1,0:T(8,128)S(1)} %get-tuple-element.5), channel_id=1, source_target_pairs={{1,0},{2,1},{3,2},{4,3},{5,4},{6,5},{7,6},{8,7},{9,8},{10,9},{11,1... | collective-permute-start | bytes 221192 | tf_op jit(solution)/shard_map/ppermute | solution.py:150
  5.8 1.3 %collective-permute-start.3 = (f32[16,3]{0,1:T(4,128)S(1)}, f32[16,3]{0,1:T(4,128)S(1)}, u32[]{:S(2)}, u32[]{:S(2)}) collective-permute-start(f32[16,3]{0,1:T(4,128)S(1)} %get-tuple-element.8), channel_id=1, source_target_pairs={{1,0},{2,1},{3,2},{4,3},{5,4},{6,5},{7,6},{8,7},{9,8},{10,9},{11,1... | collective-permute-start | bytes 584 | tf_op jit(solution)/shard_map/ppermute | solution.py:152
  7.1 5.8 %collective-permute-start.2 = (f32[16,3]{0,1:T(4,128)S(1)}, f32[16,3]{0,1:T(4,128)S(1)}, u32[]{:S(2)}, u32[]{:S(2)}) collective-permute-start(f32[16,3]{0,1:T(4,128)S(1)} %get-tuple-element.7), channel_id=1, source_target_pairs={{0,1},{1,2},{2,3},{3,4},{4,5},{5,6},{6,7},{7,8},{8,9},{9,10},{10,1... | collective-permute-start | bytes 584 | tf_op jit(solution)/shard_map/ppermute | solution.py:151
  13.1 0.6 copy-done
  13.7 0.4 fusion.10
  14.1 0.8 reshape.137
  14.9 7.3 %all-to-all-start.1 = ((f32[16,1,768]{2,1,0:T(1,128)}), f32[16,1,768]{2,1,0:T(1,128)S(1)}, u32[]{:S(2)}, u32[]{:S(2)}) async-start(f32[16,1,768]{2,1,0:T(1,128)} %reshape.137), calls=%async_computation.1 | async-start | bytes 98304 | tf_op jit(solution)/shard_map/all_to_all | solution.py:183
  22.2 0.6 dynamic_slice.12
  22.9 1.2 %compare_convert_fusion.live = f32[1,256]{1,0:T(1,128)} fusion(s32[]{:T(128)} %bitcast.8), kind=kLoop, calls=%fused_computation.40 | loop fusion | flops 512 | bytes 1028 | tf_op jit(solution)/shard_map/convert_element_type | solution.py:163
  24.1 0.6 compare_convert_fusion.1
  24.8 0.9 pad.12.own
  25.7 0.9 %copy-done.2 = f32[3,125,125]{2,1,0:T(8,128)S(1)} copy-done((f32[3,125,125]{2,1,0:T(8,128)S(1)}, f32[3,125,125]{2,1,0:T(8,128)}, u32[]{:S(2)}) %copy-start.2) | copy-done | bytes 187524
  26.8 0.8 pad.13.clone
  27.8 0.7 pad.14.weight
  28.6 0.4 select_reduce_fusion
  29.3 0.7 reshape.128.cpl
  30.2 0.8 broadcast_in_dim.29.metric
  31.0 0.7 broadcast_in_dim.30.mask
  31.7 38.2 %waves.1 = f32[48,256]{1,0:T(8,128)} custom-call(f32[9,128,128]{2,1,0:T(8,128)} %pad.12.own, f32[9,16,128]{2,1,0:T(8,128)} %copy-done.9, f32[9,16,128]{2,1,0:T(8,128)} %copy-done.10, f32[3,160,128]{2,1,0:T(8,128)} %broadcast_in_dim.29.metric, f32[160,128]{1,0:T(8,128)} %broadcast_in_dim.30.mask, f32[640,128]{1,0:T(8,128)} %bitcast.32, ...), custom_call_target="tpu_custom_call" | custom-call | flops 10000000000 | bytes 2000000 | tf_op jit(solution)/shard_map/waves/pallas_call | solution.py:114
  70.0 1.1 %fusion.7 = f32[256,48]{1,0:T(8,128)S(1)} fusion(f32[48,256]{1,0:T(8,128)} %waves.1, s32[256]{0:T(256)S(1)} %eq.75), kind=kOutput, calls=%fused_computation.12 | convolution fusion | flops 37814272 | bytes 99328 | tf_op jit(solution)/shard_map/dot_general | solution.py:191
  71.1 0.8 reshape.135
  71.9 6.0 %all-to-all-start = ((f32[16,1,768]{2,1,0:T(1,128)}), f32[16,1,768]{2,1,0:T(1,128)S(1)}, u32[]{:S(2)}, u32[]{:S(2)}) async-start(f32[16,1,768]{2,1,0:T(1,128)} %reshape.135), calls=%async_computation | async-start | bytes 98304 | tf_op jit(solution)/shard_map/all_to_all | solution.py:183
  77.9 0.5 broadcast.115
  78.4 0.8 reduce.1
  79.3 0.7 copy-done.1
  80.4 0.6 broadcast_multiply_fusion
  81.1 3.6 %all-to-all-done = f32[16,1,768]{2,1,0:T(1,128)S(1)} async-done(((f32[16,1,768]{2,1,0:T(1,128)}), f32[16,1,768]{2,1,0:T(1,128)S(1)}, u32[]{:S(2)}, u32[]{:S(2)}) %all-to-all-start) | async-done | bytes 49184 | tf_op jit(solution)/shard_map/all_to_all | solution.py:183
  84.7 0.8 reduce
  85.5 1.0 %multiply_reduce_fusion = (f32[256]{0:T(256)S(1)}, f32[256,48]{0,1:T(8,128)}) fusion(f32[256,48]{0,1:T(8,128)S(1)} %copy-done, f32[256,48]{1,0:T(8,128)S(1)} %bitcast.28, s32[256]{0:T(256)S(1)} %multiply_add_fusion, f32[256]{0:T(256)S(1)} %compare_convert_fusion.2), kind=kOutput, calls=%fused_computation.25 | convolution fusion | flops 37863168 | bytes 150528 | tf_op jit(solution)/shard_map/dot_general | solution.py:192
  86.5 0.6 broadcast_multiply_fusion.1
  (48 shorter events, 2.2 us)
Async XLA Ops:
  2.0 3.7 %copy-start.5 = (f32[3,128]{1,0:T(4,128)S(1)}, f32[3,128]{1,0:T(4,128)}, u32[]{:S(2)}) copy-start(f32[3,128]{1,0:T(4,128)} %param.14) | copy-start | bytes 4612
  2.0 10.9 %copy-start.7 = (s32[4096]{0:T(1024)S(1)}, s32[4096]{0:T(1024)}, u32[]{:S(2)}) copy-start(s32[4096]{0:T(1024)} %param.18) | copy-start | bytes 49156
  2.0 28.2 %collective-permute-start = (f32[9,16,128]{2,1,0:T(8,128)S(1)}, f32[9,16,128]{2,1,0:T(8,128)S(1)}, u32[]{:S(2)}, u32[]{:S(2)}) collective-permute-start(f32[9,16,128]{2,1,0:T(8,128)S(1)} %get-tuple-element.6), channel_id=1, source_target_pairs={{0,1},{1,2},{2,3},{3,4},{4,5},{5,6},{6,7},{7,8},{8,9},{9,10},{10,1... | collective-permute-start | bytes 221192 | tf_op jit(solution)/shard_map/ppermute | solution.py:149
  4.4 25.8 %collective-permute-start.1 = (f32[9,16,128]{2,1,0:T(8,128)S(1)}, f32[9,16,128]{2,1,0:T(8,128)S(1)}, u32[]{:S(2)}, u32[]{:S(2)}) collective-permute-start(f32[9,16,128]{2,1,0:T(8,128)S(1)} %get-tuple-element.5), channel_id=1, source_target_pairs={{1,0},{2,1},{3,2},{4,3},{5,4},{6,5},{7,6},{8,7},{9,8},{10,9},{11,1... | collective-permute-start | bytes 221192 | tf_op jit(solution)/shard_map/ppermute | solution.py:150
  5.8 24.3 %collective-permute-start.3 = (f32[16,3]{0,1:T(4,128)S(1)}, f32[16,3]{0,1:T(4,128)S(1)}, u32[]{:S(2)}, u32[]{:S(2)}) collective-permute-start(f32[16,3]{0,1:T(4,128)S(1)} %get-tuple-element.8), channel_id=1, source_target_pairs={{1,0},{2,1},{3,2},{4,3},{5,4},{6,5},{7,6},{8,7},{9,8},{10,9},{11,1... | collective-permute-start | bytes 584 | tf_op jit(solution)/shard_map/ppermute | solution.py:152
  7.1 23.0 %collective-permute-start.2 = (f32[16,3]{0,1:T(4,128)S(1)}, f32[16,3]{0,1:T(4,128)S(1)}, u32[]{:S(2)}, u32[]{:S(2)}) collective-permute-start(f32[16,3]{0,1:T(4,128)S(1)} %get-tuple-element.7), channel_id=1, source_target_pairs={{0,1},{1,2},{2,3},{3,4},{4,5},{5,6},{6,7},{7,8},{8,9},{9,10},{10,1... | collective-permute-start | bytes 584 | tf_op jit(solution)/shard_map/ppermute | solution.py:151
  12.9 0.8 copy-start
  14.9 7.3 %copy-start.8 = (s32[16]{0:T(128)S(1)}, s32[16]{0:T(128)}, u32[]{:S(2)}) copy-start(s32[16]{0:T(128)} %param.17) | copy-start | bytes 196
  14.9 57.0 %all-to-all-start.1 = ((f32[16,1,768]{2,1,0:T(1,128)}), f32[16,1,768]{2,1,0:T(1,128)S(1)}, u32[]{:S(2)}, u32[]{:S(2)}) async-start(f32[16,1,768]{2,1,0:T(1,128)} %reshape.137), calls=%async_computation.1 | async-start | bytes 98304 | tf_op jit(solution)/shard_map/all_to_all | solution.py:183
  24.8 0.9 %copy-start.4 = (f32[2,125,125]{2,0,1:T(2,128)S(1)}, f32[2,125,125]{2,0,1:T(2,128)}, u32[]{:S(2)}) copy-start(f32[2,125,125]{2,0,1:T(2,128)} %param.13) | copy-start | bytes 375004
  25.6 0.9 %copy-start.2 = (f32[3,125,125]{2,1,0:T(8,128)S(1)}, f32[3,125,125]{2,1,0:T(8,128)}, u32[]{:S(2)}) copy-start(f32[3,125,125]{2,1,0:T(8,128)} %param.11) | copy-start | bytes 562504
  26.8 1.0 %copy-start.3 = (f32[125,256]{1,0:T(8,128)S(1)}, f32[125,256]{1,0:T(8,128)}, u32[]{:S(2)}) copy-start(f32[125,256]{1,0:T(8,128)} %param.16) | copy-start | bytes 384004
  28.6 0.7 copy-start.6
  30.2 0.9 copy-start.9
  30.2 0.8 copy-start.10
  71.9 12.8 %all-to-all-start = ((f32[16,1,768]{2,1,0:T(1,128)}), f32[16,1,768]{2,1,0:T(1,128)S(1)}, u32[]{:S(2)}, u32[]{:S(2)}) async-start(f32[16,1,768]{2,1,0:T(1,128)} %reshape.135), calls=%async_computation | async-start | bytes 98304 | tf_op jit(solution)/shard_map/all_to_all | solution.py:183
  79.2 0.8 copy-start.1

commit v2 on v1

v2 whole, which is shorter than its diff:
```python
import functools
import jax
import jax.numpy as jnp
from jax import lax
from jax.experimental import pallas as pl
from jax.experimental.pallas import tpu as pltpu
from jax.sharding import PartitionSpec as P

STEPS = 12
COMPS = 4
HALO = 16
GUARD = 8


def split(x):
    hi = x.astype(jnp.bfloat16)
    return hi, (x - hi.astype(jnp.float32)).astype(jnp.bfloat16)


def zeros(*shape):
    return jnp.zeros(shape, jnp.float32)


def ones_where(cond):
    return jnp.where(cond, 1.0, 0.0).astype(jnp.bfloat16)


def dot(a, b):
    return jnp.dot(a, b, preferred_element_type=jnp.float32)


def permute(onehot, x):
    hi = x.astype(jnp.bfloat16)
    rest = x - hi.astype(jnp.float32)
    mid = rest.astype(jnp.bfloat16)
    low = (rest - mid.astype(jnp.float32)).astype(jnp.bfloat16)
    return dot(onehot, hi) + (dot(onehot, mid) + dot(onehot, low))


def greet(peers, me):
    barrier = pltpu.get_barrier_semaphore()

    def one(off, _):
        pl.semaphore_signal(barrier, inc=1, device_id={"mx": lax.rem(me + off, peers)}, device_id_type=pl.DeviceIdType.MESH)
        return 0

    lax.fori_loop(1, peers, one, 0)
    return barrier


def start_kernel(peers, initial, metric, mats, weight_in, order, counts,
                 state, wb, ws, to_send, from_send, to_place, from_place, live,
                 pad, padw, send_sem, recv_sem):
    fields, nodes, count = initial.shape
    lanes = pad.shape[0]
    slots = order.shape[1]
    pair = slots // peers
    me = lax.axis_index("mx")
    right, left = lax.rem(me + 1, peers), lax.rem(me + peers - 1, peers)
    barrier = pltpu.get_barrier_semaphore()
    for side in (left, right):
        pl.semaphore_signal(barrier, inc=1, device_id={"mx": side}, device_id_type=pl.DeviceIdType.MESH)
    pad[...] = zeros(lanes, lanes)
    for f in range(fields):
        pad[0:nodes, :] = initial[f]
        state[f, HALO:HALO + count] = pad[...].T
    kinds = metric.shape[0]
    for k in range(kinds):
        state[fields + k, HALO:HALO + count] = jnp.broadcast_to(metric[k:k + 1, :], (lanes, count)).T
    pl.semaphore_wait(barrier, 2)
    moved = fields + kinds
    copies = []
    for i, (side, at, to) in enumerate(((right, count, 0), (left, HALO, HALO + count))):
        copies.append(pltpu.make_async_remote_copy(
            src_ref=state.at[0:moved, at:at + HALO], dst_ref=state.at[0:moved, to:to + HALO],
            send_sem=send_sem.at[i], recv_sem=recv_sem.at[i],
            device_id={"mx": side}, device_id_type=pl.DeviceIdType.MESH))
        copies[-1].start()
    pad[...] = zeros(lanes, lanes)
    kdim = mats.shape[0] * lanes
    for k in range(mats.shape[0]):
        pad[0:nodes, 0:nodes] = mats[k]
        hi, lo = split(pad[...].T * (0.5 / STEPS))
        for base in (0, kdim):
            wb[base + k * lanes:base + (k + 1) * lanes, :lanes] = hi
            wb[base + k * lanes:base + (k + 1) * lanes, lanes:] = lo
    padw[...] = zeros(lanes, slots)
    padw[0:nodes, :] = weight_in[...]
    hi, lo = split(padw[...])
    ws[0:lanes] = hi
    ws[lanes:2 * lanes] = hi
    ws[2 * lanes:] = lo
    rows = lax.broadcasted_iota(jnp.int32, (count + 2 * HALO, lanes), 0) + (me * count - HALO)
    state[moved] = jnp.where((rows >= 0) & (rows < count * peers), 1.0, 0.0)

    up = lax.broadcasted_iota(jnp.int32, (slots, slots), 0)
    across = lax.broadcasted_iota(jnp.int32, (slots, slots), 1)
    tri = ones_where(up <= across)
    blocks = order[...]
    source, slot = lax.div(blocks, slots), lax.rem(blocks, slots)
    mine = source == me
    rank = dot(ones_where(mine), tri) - 1.0
    rank = jnp.where(mine, rank, -1.0)
    tall = lax.broadcasted_iota(jnp.int32, (slots, peers), 0)
    wide = lax.broadcasted_iota(jnp.int32, (slots, peers), 1)
    repeat = ones_where(lax.div(tall, pair) == wide)
    rank_all = dot(repeat, rank.astype(jnp.bfloat16))
    slot_all = dot(repeat, slot.astype(jnp.float32).astype(jnp.bfloat16))
    hit = rank_all == lax.rem(up, pair).astype(jnp.float32)
    send_slot = jnp.sum(jnp.where(hit, slot_all, 0.0), axis=1, keepdims=True)
    sends = jnp.where(send_slot == across.astype(jnp.float32), 1.0, 0.0)
    to_send[...] = sends.astype(jnp.bfloat16)
    from_send[...] = sends.T.astype(jnp.bfloat16)
    own = order[pl.ds(me, 1), :]
    own_source = lax.div(own, slots)
    peer_ids = lax.broadcasted_iota(jnp.int32, (peers, slots), 0)
    from_peer = peer_ids == own_source
    seen = dot(ones_where(from_peer), tri) - 1.0
    own_rank = jnp.sum(jnp.where(from_peer, seen, 0.0), axis=0, keepdims=True)
    place = own_source.astype(jnp.float32) * float(pair) + own_rank
    places = jnp.where(up.astype(jnp.float32) == place, 1.0, 0.0)
    to_place[...] = places.astype(jnp.bfloat16)
    from_place[...] = places.T.astype(jnp.bfloat16)
    limit = counts[pl.ds(me, 1), :]
    live[...] = jnp.where(lax.broadcasted_iota(jnp.int32, (1, slots), 1) < limit, 1.0, 0.0)
    for copy in copies:
        copy.wait()


def end_kernel(peers, traces, observed, to_send, from_send, to_place, from_place,
               residual, misfit, adjoint, sent, got, send_sem, recv_sem):
    slots, width = observed.shape
    lanes = sent.shape[-1]
    wide = traces.shape[0]
    pair = slots // peers
    me = lax.axis_index("mx")
    barrier = greet(peers, me)
    synth = traces[...].T
    packed = permute(to_send[...], synth)
    obs = permute(to_place[...], observed[...])
    row = jnp.concatenate([packed, obs, zeros(slots, lanes - wide - width)], axis=1)
    sent[...] = row.reshape(peers, pair, lanes)
    pl.semaphore_wait(barrier, peers - 1)

    def copy_to(off):
        dest = lax.rem(me + off, peers)
        return pltpu.make_async_remote_copy(
            src_ref=sent.at[dest], dst_ref=got.at[me], send_sem=send_sem.at[dest], recv_sem=recv_sem.at[me],
            device_id={"mx": dest}, device_id_type=pl.DeviceIdType.MESH)

    def copy_from(off):
        src = lax.rem(me - off + peers, peers)
        return pltpu.make_async_remote_copy(
            src_ref=sent.at[src], dst_ref=got.at[src], send_sem=send_sem.at[src], recv_sem=recv_sem.at[src],
            device_id={"mx": src}, device_id_type=pl.DeviceIdType.MESH)

    def begin(off, _):
        copy_to(off).start()
        return 0

    def finish(off, _):
        copy_from(off).wait_recv()
        return 0

    def drain(off, _):
        copy_to(off).wait_send()
        return 0

    lax.fori_loop(1, peers, begin, 0)
    got[pl.ds(me, 1)] = sent[pl.ds(me, 1)]
    lax.fori_loop(1, peers, finish, 0)
    arrived = got[...].reshape(slots, lanes)
    placed = permute(from_place[...], arrived[:, :wide])
    res = placed[:, width:width + 1] * (placed[:, :width] - observed[...])
    residual[...] = res
    misfit[...] = 0.5 * jnp.sum(res * res, axis=1, keepdims=True)
    slot_obs = permute(from_send[...], arrived[:, wide:wide + width])
    plain = synth[:, width:width + 1] * (synth[:, :width] - slot_obs)
    a = lax.broadcasted_iota(jnp.int32, (width, width), 0)
    b = lax.broadcasted_iota(jnp.int32, (width, width), 1)
    back = ones_where((lax.div(a, STEPS) == lax.div(b, STEPS)) & (lax.rem(a, STEPS) + lax.rem(b, STEPS) == STEPS - 1))
    hi = plain.astype(jnp.bfloat16)
    rest = plain - hi.astype(jnp.float32)
    mid = rest.astype(jnp.bfloat16)
    low = (rest - mid.astype(jnp.float32)).astype(jnp.bfloat16)
    adjoint[...] = dot(hi, back) + (dot(mid, back) + dot(low, back))
    lax.fori_loop(1, peers, drain, 0)


def wave_kernel(state, wb, ws, elem, live, cpl, out, ubuf, lhs, hist):
    fields = ubuf.shape[1]
    lanes = state.shape[2]
    count = state.shape[1] - 2 * HALO
    first = GUARD + HALO
    kdim = wb.shape[0] // 2
    rows_all = ubuf.shape[2]
    metric = state.at[fields:fields + 3]
    mask = state.at[fields + 3]
    for b in range(2):
        for f in range(fields):
            ubuf[b, f, 0:GUARD] = zeros(GUARD, lanes)
            ubuf[b, f, rows_all - GUARD:] = zeros(GUARD, lanes)
            if b:
                ubuf[b, f] = zeros(rows_all, lanes)
            else:
                ubuf[b, f, GUARD:rows_all - GUARD] = state[f] * mask[...]

    def mix(src, c, halo, slab):
        rows = count + 2 * halo
        base = first - halo
        for gi in range(3):
            g = c * 3 + gi
            for r in range(0, rows, slab):
                acc = [None] * 3
                for f in range(fields):
                    uf = ubuf[src, f, base + r:base + r + slab]
                    for k in range(3):
                        term = cpl[(k * fields + g) * fields + f] * uf
                        acc[k] = term if acc[k] is None else acc[k] + term
                at = gi * rows + r
                mid = ubuf[src, g, base + r:base + r + slab]
                vals = [acc[k] * metric[k, HALO - halo + r:HALO - halo + r + slab] for k in range(3)]
                vals.append(ubuf[src, g, base + r - 1:base + r - 1 + slab] - mid)
                vals.append(ubuf[src, g, base + r + 1:base + r + 1 + slab] - mid)
                for k, v in enumerate(vals):
                    hi, lo = split(v)
                    lhs[c, at:at + slab, k * lanes:(k + 1) * lanes] = hi
                    lhs[c, at:at + slab, kdim + k * lanes:kdim + (k + 1) * lanes] = lo

    def apply(src, dst, c, halo):
        rows = count + 2 * halo
        base = first - halo
        res = jnp.dot(lhs[c, :3 * rows], wb[...], preferred_element_type=jnp.float32)
        for gi in range(3):
            g = c * 3 + gi
            part = res[gi * rows:(gi + 1) * rows]
            new = ubuf[src, g, base:base + rows] + (part[:, :lanes] + part[:, lanes:])
            ubuf[dst, g, base:base + rows] = new * mask[HALO - halo:HALO - halo + rows]

    def step(halo, slab, t, _):
        src = lax.rem(t, 2)
        dst = 1 - src
        mix(src, 0, halo, slab)
        mix(src, 1, halo, slab)
        apply(src, dst, 0, halo)
        mix(src, 2, halo, slab)
        apply(src, dst, 1, halo)
        apply(src, dst, 2, halo)
        mine = slice(first, first + count)
        vals = [ubuf[dst, c, mine] for c in range(3)]
        vals.append((ubuf[dst, 3, mine] + ubuf[dst, 4, mine] + ubuf[dst, 5, mine]) / 3.0)
        for c, v in enumerate(vals):
            hi, lo = split(v)
            hist[t, c, :, 0:lanes] = hi
            hist[t, c, :, lanes:2 * lanes] = lo
            hist[t, c, :, 2 * lanes:] = hi
        return 0

    lax.fori_loop(0, 3, functools.partial(step, 16, 80), 0)
    lax.fori_loop(3, STEPS, functools.partial(step, 8, 48), 0)

    slots = ws.shape[1]
    ids = lax.broadcasted_iota(jnp.int32, (count, slots), 0)
    pick = jnp.where(ids == elem[...], live[...], 0.0)

    out[...] = zeros(*out.shape)
    out[COMPS * STEPS:COMPS * STEPS + 1, :] = live[...]

    def sample(t, _):
        for c in range(COMPS):
            prod = jnp.dot(hist[t, c], ws[...], preferred_element_type=jnp.float32)
            out[pl.ds(c * STEPS + t, 1), :] = jnp.sum(prod * pick, axis=0, keepdims=True)
        return 0

    lax.fori_loop(0, STEPS, sample, 0)


VM = pl.BlockSpec(memory_space=pltpu.VMEM)


def shards(initial, derivative, coupling, face_lift, metric, rec_element, rec_weight, live_counts, shot_order, observed):
    fields, nodes, count = initial.shape
    lanes = -(-nodes // 128) * 128
    slots, width = observed.shape
    peers = lax.axis_size("mx")
    mats = jnp.concatenate([derivative, face_lift], axis=0)
    span = count + 2 * HALO
    kdim = mats.shape[0] * lanes
    wide = -(-(width + 1) // 64) * 64
    f32, bf16 = jnp.float32, jnp.bfloat16
    square = jax.ShapeDtypeStruct((slots, slots), bf16)
    state, wb, ws, to_send, from_send, to_place, from_place, live = pl.pallas_call(
        functools.partial(start_kernel, peers),
        out_shape=(
            jax.ShapeDtypeStruct((fields + metric.shape[0] + 1, span, lanes), f32),
            jax.ShapeDtypeStruct((2 * kdim, 2 * lanes), bf16),
            jax.ShapeDtypeStruct((3 * lanes, slots), bf16),
            square, square, square, square,
            jax.ShapeDtypeStruct((1, slots), f32),
        ),
        in_specs=[VM] * 6,
        out_specs=[VM] * 8,
        scratch_shapes=[
            pltpu.VMEM((lanes, lanes), f32),
            pltpu.VMEM((lanes, slots), f32),
            pltpu.SemaphoreType.DMA((2,)),
            pltpu.SemaphoreType.DMA((2,)),
        ],
        compiler_params=pltpu.CompilerParams(collective_id=0, has_side_effects=True),
        name="start",
    )(initial, metric, mats, rec_weight, shot_order.reshape(peers, slots), live_counts[:, None])
    traces = pl.pallas_call(
        wave_kernel,
        out_shape=jax.ShapeDtypeStruct((wide, slots), f32),
        in_specs=[VM] * 5 + [pl.BlockSpec(memory_space=pltpu.SMEM)],
        out_specs=VM,
        scratch_shapes=[
            pltpu.VMEM((2, fields, span + 2 * GUARD, lanes), f32),
            pltpu.VMEM((3, 3 * span, 2 * kdim), bf16),
            pltpu.VMEM((STEPS, COMPS, count, 3 * lanes), bf16),
        ],
        name="waves",
    )(state, wb, ws, rec_element[None, :], live, coupling.reshape(-1))
    residual, misfit, adjoint = pl.pallas_call(
        functools.partial(end_kernel, peers),
        out_shape=(
            jax.ShapeDtypeStruct((slots, width), f32),
            jax.ShapeDtypeStruct((slots, 1), f32),
            jax.ShapeDtypeStruct((slots, width), f32),
        ),
        in_specs=[VM] * 6,
        out_specs=[VM] * 3,
        scratch_shapes=[
            pltpu.VMEM((peers, slots // peers, lanes), f32),
            pltpu.VMEM((peers, slots // peers, lanes), f32),
            pltpu.SemaphoreType.DMA((peers,)),
            pltpu.SemaphoreType.DMA((peers,)),
        ],
        compiler_params=pltpu.CompilerParams(collective_id=1, has_side_effects=True),
        name="finish",
    )(traces, observed, to_send, from_send, to_place, from_place)
    return residual, misfit[:, 0], adjoint


def solution(mesh):
    in_specs = (
        P("shots", None, "mx"),
        P(),
        P(),
        P(),
        P(None, "mx"),
        P("mx"),
        P(None, "mx"),
        P(),
        P(),
        P(("shots", "mx"), None),
    )
    out_specs = (P(("shots", "mx"), None), P(("shots", "mx")), P(("shots", "mx"), None))
    return jax.shard_map(shards, mesh=mesh, in_specs=in_specs, out_specs=out_specs, check_vma=False)
```

time: 87.8 us -> 72 us (0.82)
  starting transfers between devices: 24.1 us -> 0 us
  Pallas kernels: 38.2 us -> 59.5 us
  local copies, waits for them, and re-layouts: 11.9 us -> 8.19 us
  waiting for transfers between devices: 3.61 us -> 0 us
  matrix products: 3.07 us -> 0 us
  other arithmetic: 5.18 us -> 3.29 us
    pallas_call x1 -> x3, Pallas kernels: 38.2 us -> 59.5 us  [the longest x1 38.3 us: shards(): pl.pallas_call(wave_kernel, out_shape=jax.ShapeDtypeStruct((wide, slots),...]
    all_to_all x2 -> x0, starting transfers between devices: 13.3 us -> none  [exchange(): lax.all_to_all(rows.reshape(peers, pair, -1), 'mx', split_axis=0, concat_...]
    ppermute x4 -> x0, starting transfers between devices: 10.8 us -> none  [the longest x1 5.78 us: shards(): met_low = lax.ppermute(met[elems - HALO:], 'mx', up)]
    all_to_all x2 -> x0, waiting for transfers between devices: 3.6 us -> none  [exchange(): lax.all_to_all(rows.reshape(peers, pair, -1), 'mx', split_axis=0, concat_...]
    dot_general x6 -> x0, matrix products: 3.07 us -> none  [the longest x1 1.1 us: shards(): lax.dot_general(to_send, traces, (((1,), (1,)), ((), ())), precision=HIGH)]
    pad x3 -> x0, local copies, waits for them, and re-layouts: 2.28 us -> none  [the longest x1 0.87 us: shards(): own = jnp.pad(initial.transpose(0, 2, 1), ((0, 0), (0, 0), (0, pad)))]
    convert_element_type x4 -> x0, other arithmetic: 1.87 us -> none  [the longest x2 1.86 us: shards(): live = (slot_ids < live_counts[me]).astype(jnp.float32)]
    concatenate x0 -> x1, other arithmetic: none -> 1.71 us  [shards(): mats = jnp.concatenate([derivative, face_lift], axis=0)]
  transfers between devices with their start and end apart: 6 -> 0, of which waited for: 1 -> 0; matrix products, arithmetic and copies ran while one was open for 16% -> 0% of each run, Pallas kernels for 44% -> 0%
where the time goes in v2:
time: 72 us; the launch traced here: 71.6 us
  Pallas kernels  59.5 us (83%)
  local copies, waits for them, and re-layouts  8.19 us (11%)
  other arithmetic  3.29 us (5%)
    pallas_call x1, Pallas kernels, shards(): pl.pallas_call(wave_kernel, out_shape=jax.ShapeDtypeStruct((wide, slots),...  38.3 us
    pallas_call x1, Pallas kernels, shards(): pl.pallas_call(functools.partial(start_kernel, peers), out_shape=(jax.Sha...  11.2 us
    pallas_call x1, Pallas kernels, shards(): pl.pallas_call(functools.partial(end_kernel, peers), out_shape=(jax.Shape...  10 us
    unnamed x9, local copies, waits for them, and re-layouts  4.87 us
    concatenate x1, other arithmetic, shards(): mats = jnp.concatenate([derivative, face_lift], axis=0)  1.71 us
    pallas_call x1, other arithmetic, shards(): pl.pallas_call(functools.partial(end_kernel, peers), out_shape=(jax.Shape...  1.58 us

profile of v2, /device:TPU:0, one launch (start us, length us, event | category | flops | bytes accessed | tf_op | source)
XLA Modules:
  0.0 71.6 jit_solution(14403206728041193284)
XLA Ops:
  0.6 0.0 copy-start.1
  0.6 0.9 %copy.18 = f32[2,125,125]{2,1,0:T(8,128)S(1)} copy(f32[2,125,125]{2,0,1:T(2,128)} %param.13) | data formatting | bytes 250000 | tf_op args[3]
  1.6 1.7 %pad_maximum_fusion.mats = f32[5,125,125]{2,1,0:T(8,128)} fusion(f32[2,125,125]{2,1,0:T(8,128)S(1)} %copy.18, f32[3,125,125]{2,1,0:T(8,128)} %param.11), kind=kLoop, calls=%fused_computation | loop fusion | flops 78125 | bytes 625000 | tf_op jit(solution)/shard_map/concatenate | solution.py:286
  3.3 1.3 %reshape.12.order = s32[16,256]{1,0:T(8,128)} reshape(s32[4096]{0:T(1024)} %param.18) | data formatting | bytes 32768 | tf_op jit(solution)/shard_map/reshape | solution.py:311
  4.6 1.3 %copy.19.counts = s32[16,1]{1,0:T(8,128)} copy(s32[16,1]{0,1:T(1,128)} %bitcast.3) | data formatting | bytes 128 | tf_op jit(solution)/shard_map/broadcast_in_dim | solution.py:311
  5.9 11.2 %start.1 = (f32[13,160,128]{2,1,0:T(8,128)}, bf16[1280,256]{1,0:T(8,128)(2,1)}, bf16[384,256]{1,0:T(8,128)(2,1)}, bf16[256,256]{1,0:T(8,128)(2,1)}, bf16[256,256...) custom-call(f32[9,125,128]{2,1,0:T(8,128)} %initial.1, ...), custom_call_target="tpu_custom_call" | custom-call | tf_op jit(solution)/shard_map/start/pallas_call | solution.py:292
  17.2 0.0 copy-start
  17.2 0.0 copy-done.1
  17.2 0.7 reshape.13.cpl
  17.9 38.3 %waves.1.traces = f32[64,256]{1,0:T(8,128)} custom-call(f32[13,160,128]{2,1,0:T(8,128)} %get-tuple-element.14.state, bf16[1280,256]{1,0:T(8,128)(2,1)} %get-tuple-element.15.wb, bf16[384,256]{1,0:T(8,128)(2,1)} %get-tuple-element.16.ws, s32[1,256]{1,0:T(1,128)} %bitcast.2, f32[1,256]{1,0:T(1,128)} %get-tuple-element.17.live, f32[243]{0:T(256)} %reshape.13.cpl), custom_call_target="tpu_custom_call" | custom-call | tf_op jit(solution)/shard_map/waves/pallas_call | solution.py:312
  56.1 0.0 copy-done
  56.1 0.7 %copy.21.observed = f32[256,48]{1,0:T(8,128)} copy(f32[256,48]{0,1:T(8,128)S(1)} %copy-done) | data formatting | bytes 98304 | tf_op args[9]
  56.8 10.0 %finish.1 = (f32[256,48]{1,0:T(8,128)}, f32[256,1]{1,0:T(8,128)}, f32[256,48]{1,0:T(8,128)}) custom-call(f32[64,256]{1,0:T(8,128)} %waves.1.traces, f32[256,48]{1,0:T(8,128)} %copy.21.observed, bf16[256,256]{1,0:T(8,128)(2,1)} %get-tuple-element.18.to_send, bf16[256,256]{1,0:T(8,128)(2,1)} %get-tuple-element.19.from_send, ...), custom_call_target="tpu_custom_call" | custom-call | tf_op jit(solution)/shard_map/finish/pallas_call | solution.py:324
  66.9 1.6 %copy.22 = f32[256,48]{0,1:T(8,128)} copy(f32[256,48]{1,0:T(8,128)} %get-tuple-element.28) | data formatting | bytes 98304
  68.5 1.6 %copy.23 = f32[256,48]{0,1:T(8,128)} copy(f32[256,48]{1,0:T(8,128)} %get-tuple-element.30) | data formatting | bytes 98304
  70.1 1.6 %reduce = f32[256]{0:T(256)} reduce(f32[256,1]{1,0:T(8,128)} %get-tuple-element.23, f32[]{:T(128)} %constant.1), dimensions={1}, to_apply=%get-tuple-element.23.reduce_sub_computation | reduce | bytes 2052 | tf_op jit(solution)/shard_map/finish/pallas_call | solution.py:324
  (1 shorter events, 0.0 us)
Async XLA Ops:
  0.6 16.5 %copy-start.1 = (f32[3,9,9]{2,0,1:T(4,128)S(1)}, f32[3,9,9]{2,0,1:T(4,128)}, u32[]{:S(2)}) copy-start(f32[3,9,9]{2,0,1:T(4,128)} %param.12) | copy-start | bytes 2920
  17.2 39.0 %copy-start = (f32[256,48]{0,1:T(8,128)S(1)}, f32[256,48]{0,1:T(8,128)}, u32[]{:S(2)}) copy-start(f32[256,48]{0,1:T(8,128)} %param.19) | copy-start | bytes 147460

commit v3 on v2

--- a/solution.py
+++ b/solution.py
@@ -48,7 +48,7 @@
     return barrier
 
 
-def start_kernel(peers, initial, metric, mats, weight_in, order, counts,
+def start_kernel(peers, initial, metric, derivative, face_lift, weight_in, order, counts,
                  state, wb, ws, to_send, from_send, to_place, from_place, live,
                  pad, padw, send_sem, recv_sem):
     fields, nodes, count = initial.shape
@@ -77,9 +77,10 @@
             device_id={"mx": side}, device_id_type=pl.DeviceIdType.MESH))
         copies[-1].start()
     pad[...] = zeros(lanes, lanes)
-    kdim = mats.shape[0] * lanes
-    for k in range(mats.shape[0]):
-        pad[0:nodes, 0:nodes] = mats[k]
+    turns = derivative.shape[0]
+    kdim = (turns + face_lift.shape[0]) * lanes
+    for k in range(kdim // lanes):
+        pad[0:nodes, 0:nodes] = derivative[k] if k < turns else face_lift[k - turns]
         hi, lo = split(pad[...].T * (0.5 / STEPS))
         for base in (0, kdim):
             wb[base + k * lanes:base + (k + 1) * lanes, :lanes] = hi
@@ -121,15 +122,16 @@
     places = jnp.where(up.astype(jnp.float32) == place, 1.0, 0.0)
     to_place[...] = places.astype(jnp.bfloat16)
     from_place[...] = places.T.astype(jnp.bfloat16)
-    limit = counts[pl.ds(me, 1), :]
-    live[...] = jnp.where(lax.broadcasted_iota(jnp.int32, (1, slots), 1) < limit, 1.0, 0.0)
+    here = lax.broadcasted_iota(jnp.int32, (1, peers), 1) == me
+    limit = jnp.sum(jnp.where(here, counts[...].astype(jnp.float32), 0.0), axis=1, keepdims=True)
+    live[...] = jnp.where(lax.broadcasted_iota(jnp.int32, (1, slots), 1).astype(jnp.float32) < limit, 1.0, 0.0)
     for copy in copies:
         copy.wait()
 
 
 def end_kernel(peers, traces, observed, to_send, from_send, to_place, from_place,
                residual, misfit, adjoint, sent, got, send_sem, recv_sem):
-    slots, width = observed.shape
+    width, slots = observed.shape
     lanes = sent.shape[-1]
     wide = traces.shape[0]
     pair = slots // peers
@@ -137,7 +139,7 @@
     barrier = greet(peers, me)
     synth = traces[...].T
     packed = permute(to_send[...], synth)
-    obs = permute(to_place[...], observed[...])
+    obs = permute(to_place[...], observed[...].T)
     row = jnp.concatenate([packed, obs, zeros(slots, lanes - wide - width)], axis=1)
     sent[...] = row.reshape(peers, pair, lanes)
     pl.semaphore_wait(barrier, peers - 1)
@@ -170,20 +172,16 @@
     got[pl.ds(me, 1)] = sent[pl.ds(me, 1)]
     lax.fori_loop(1, peers, finish, 0)
     arrived = got[...].reshape(slots, lanes)
-    placed = permute(from_place[...], arrived[:, :wide])
-    res = placed[:, width:width + 1] * (placed[:, :width] - observed[...])
+    placed = permute(from_place[...], arrived[:, :wide]).T
+    res = placed[width:width + 1] * (placed[:width] - observed[...])
     residual[...] = res
-    misfit[...] = 0.5 * jnp.sum(res * res, axis=1, keepdims=True)
-    slot_obs = permute(from_send[...], arrived[:, wide:wide + width])
-    plain = synth[:, width:width + 1] * (synth[:, :width] - slot_obs)
+    misfit[...] = 0.5 * jnp.sum(res * res, axis=0, keepdims=True)
+    slot_obs = permute(from_send[...], arrived[:, wide:wide + width]).T
+    plain = traces[width:width + 1, :] * (traces[0:width, :] - slot_obs)
     a = lax.broadcasted_iota(jnp.int32, (width, width), 0)
     b = lax.broadcasted_iota(jnp.int32, (width, width), 1)
     back = ones_where((lax.div(a, STEPS) == lax.div(b, STEPS)) & (lax.rem(a, STEPS) + lax.rem(b, STEPS) == STEPS - 1))
-    hi = plain.astype(jnp.bfloat16)
-    rest = plain - hi.astype(jnp.float32)
-    mid = rest.astype(jnp.bfloat16)
-    low = (rest - mid.astype(jnp.float32)).astype(jnp.bfloat16)
-    adjoint[...] = dot(hi, back) + (dot(mid, back) + dot(low, back))
+    adjoint[...] = permute(back, plain)
     lax.fori_loop(1, peers, drain, 0)
 
 
@@ -283,9 +281,8 @@
     lanes = -(-nodes // 128) * 128
     slots, width = observed.shape
     peers = lax.axis_size("mx")
-    mats = jnp.concatenate([derivative, face_lift], axis=0)
     span = count + 2 * HALO
-    kdim = mats.shape[0] * lanes
+    kdim = (derivative.shape[0] + face_lift.shape[0]) * lanes
     wide = -(-(width + 1) // 64) * 64
     f32, bf16 = jnp.float32, jnp.bfloat16
     square = jax.ShapeDtypeStruct((slots, slots), bf16)
@@ -298,7 +295,7 @@
             square, square, square, square,
             jax.ShapeDtypeStruct((1, slots), f32),
         ),
-        in_specs=[VM] * 6,
+        in_specs=[VM] * 7,
         out_specs=[VM] * 8,
         scratch_shapes=[
             pltpu.VMEM((lanes, lanes), f32),
@@ -308,7 +305,7 @@
         ],
         compiler_params=pltpu.CompilerParams(collective_id=0, has_side_effects=True),
         name="start",
-    )(initial, metric, mats, rec_weight, shot_order.reshape(peers, slots), live_counts[:, None])
+    )(initial, metric, derivative, face_lift, rec_weight, shot_order.reshape(peers, slots), live_counts[None, :])
     traces = pl.pallas_call(
         wave_kernel,
         out_shape=jax.ShapeDtypeStruct((wide, slots), f32),
@@ -324,9 +321,9 @@
     residual, misfit, adjoint = pl.pallas_call(
         functools.partial(end_kernel, peers),
         out_shape=(
-            jax.ShapeDtypeStruct((slots, width), f32),
-            jax.ShapeDtypeStruct((slots, 1), f32),
-            jax.ShapeDtypeStruct((slots, width), f32),
+            jax.ShapeDtypeStruct((width, slots), f32),
+            jax.ShapeDtypeStruct((1, slots), f32),
+            jax.ShapeDtypeStruct((width, slots), f32),
         ),
         in_specs=[VM] * 6,
         out_specs=[VM] * 3,
@@ -338,8 +335,8 @@
         ],
         compiler_params=pltpu.CompilerParams(collective_id=1, has_side_effects=True),
         name="finish",
-    )(traces, observed, to_send, from_send, to_place, from_place)
-    return residual, misfit[:, 0], adjoint
+    )(traces, observed.T, to_send, from_send, to_place, from_place)
+    return residual.T, misfit[0], adjoint.T
 
 
 def solution(mesh):

time: 72 us -> 68 us (0.944)
  other arithmetic: 3.29 us -> 0 us
    concatenate x1 -> x0, other arithmetic: 1.71 us -> none  [shards(): mats = jnp.concatenate([derivative, face_lift], axis=0)]
    pallas_call x1 -> x0, other arithmetic: 1.58 us -> none  [shards(): pl.pallas_call(functools.partial(end_kernel, peers), out_shape=(jax.Shape...]
    broadcast_in_dim x1 -> x0, local copies, waits for them, and re-layouts: 1.33 us -> none  [shards(): live_counts[:, None]]
    unnamed x9 -> x7, local copies, waits for them, and re-layouts: 4.87 us -> 5.65 us
where the time goes in v3:
time: 68 us; the launch traced here: 67.6 us
  Pallas kernels  59.3 us (87%)
  local copies, waits for them, and re-layouts  7.64 us (11%)
    pallas_call x1, Pallas kernels, shards(): pl.pallas_call(wave_kernel, out_shape=jax.ShapeDtypeStruct((wide, slots),...  38.2 us
    pallas_call x1, Pallas kernels, shards(): pl.pallas_call(functools.partial(start_kernel, peers), out_shape=(jax.Sha...  11.2 us
    pallas_call x1, Pallas kernels, shards(): pl.pallas_call(functools.partial(end_kernel, peers), out_shape=(jax.Shape...  9.84 us
    unnamed x7, local copies, waits for them, and re-layouts  5.65 us

profile of v3, /device:TPU:0, one launch (start us, length us, event | category | flops | bytes accessed | tf_op | source)
XLA Modules:
  0.0 67.6 jit_solution(16065262305417792579)
XLA Ops:
  0.6 0.0 copy-start
  0.6 1.6 %copy.14.face_lift = f32[2,125,125]{2,1,0:T(8,128)} copy(f32[2,125,125]{2,0,1:T(2,128)} %param.13) | data formatting | bytes 250000 | tf_op args[3]
  2.2 1.3 %reshape.12.order = s32[16,256]{1,0:T(8,128)} reshape(s32[4096]{0:T(1024)} %param.18) | data formatting | bytes 32768 | tf_op jit(solution)/shard_map/reshape | solution.py:308
  3.5 11.2 %start.1 = (f32[13,160,128]{2,1,0:T(8,128)}, bf16[1280,256]{1,0:T(8,128)(2,1)}, bf16[384,256]{1,0:T(8,128)(2,1)}, bf16[256,256]{1,0:T(8,128)(2,1)}, bf16[256,256...) custom-call(f32[9,125,128]{2,1,0:T(8,128)} %initial.1, ...), custom_call_target="tpu_custom_call" | custom-call | tf_op jit(solution)/shard_map/start/pallas_call | solution.py:289
  14.7 0.0 copy-done
  14.8 0.7 reshape.13.cpl
  15.4 38.2 %waves.1.traces = f32[64,256]{1,0:T(8,128)} custom-call(f32[13,160,128]{2,1,0:T(8,128)} %get-tuple-element.14.state, bf16[1280,256]{1,0:T(8,128)(2,1)} %get-tuple-element.15.wb, bf16[384,256]{1,0:T(8,128)(2,1)} %get-tuple-element.16.ws, s32[1,256]{1,0:T(1,128)} %bitcast.9, f32[1,256]{1,0:T(1,128)} %get-tuple-element.17.live, f32[243]{0:T(256)} %reshape.13.cpl), custom_call_target="tpu_custom_call" | custom-call | tf_op jit(solution)/shard_map/waves/pallas_call | solution.py:309
  53.7 9.8 %finish.1 = (f32[48,256]{1,0:T(8,128)}, f32[1,256]{1,0:T(1,128)}, f32[48,256]{1,0:T(8,128)}) custom-call(f32[64,256]{1,0:T(8,128)} %waves.1.traces, f32[48,256]{1,0:T(8,128)} %bitcast.6, bf16[256,256]{1,0:T(8,128)(2,1)} %get-tuple-element.18.to_send, bf16[256,256]{1,0:T(8,128)(2,1)} %get-tuple-element.19.from_send, ...), custom_call_target="tpu_custom_call" | custom-call | tf_op jit(solution)/shard_map/finish/pallas_call | solution.py:321
  63.5 1.4 %copy.19 = f32[256,48]{0,1:T(8,128)} copy(f32[256,48]{0,1:T(8,128)} %bitcast.8) | data formatting | bytes 98304
  64.9 1.2 %copy.20 = f32[256]{0:T(256)} copy(f32[256]{0:T(256)} %bitcast.10) | data formatting | bytes 2048
  66.2 1.4 %copy.21 = f32[256,48]{0,1:T(8,128)} copy(f32[256,48]{0,1:T(8,128)} %bitcast.7) | data formatting | bytes 98304
  (1 shorter events, 0.0 us)
Async XLA Ops:
  0.6 14.1 %copy-start = (f32[3,9,9]{2,0,1:T(4,128)S(1)}, f32[3,9,9]{2,0,1:T(4,128)}, u32[]{:S(2)}) copy-start(f32[3,9,9]{2,0,1:T(4,128)} %param.12) | copy-start | bytes 2920
